TPU v7x, 256 devices: a whole 4x4x8 slice. The times are simulated.
256 devices in a mesh: band: 16 (over y_hi, z), grid: 16 (over y_lo, x, core).
Axes of the slice: x: 4, y: 4 (y_hi: 2, y_lo: 2; y = y_hi * 2 + y_lo), z: 8, core: 2. Of those that a mesh axis runs over, the one named last changes fastest.
Arguments:
- own_bands: float32 [64, 128, 128, 128], P('band', 'grid'), may hold values from -1.5 to 1.5
- travel_bands: float32 [64, 128, 128, 128], P('band', 'grid'), may hold values from -1.5 to 1.5
Outputs:
- own_terms: float32 [64, 128, 128, 128], P('band', 'grid')
- partner_terms: float32 [64, 128, 128, 128], P('band', 'grid')
All inputs are finite; a program needn't handle non-finite values.
Results may differ from a plain program's by a relative error of at most 0.00011.
Values sent between devices are 32-bit elements; how exact they have to be, the bound alone decides.
A program may use at most 64 MiB of HBM per device.

v0:
```python
import math

import jax
import jax.numpy as jnp
from jax import lax
from jax.sharding import PartitionSpec as P

NX = 128
NY = 128
NZ = 128


FRACTION = 0.25
HIGHEST_PRECISION = lax.Precision.HIGHEST


def passed_along(block, axis, distance):
    devices = range(lax.axis_size(axis))
    route = [((i - distance) % len(devices), i) for i in devices]
    return lax.ppermute(block, axis, route)


def wave_square(points, first_row, length):
    position = first_row + jnp.arange(points, dtype=jnp.int32)
    position = (position + length // 2) % length - length // 2
    wavenumber = 2.0 * math.pi / length * position.astype(jnp.float32)
    return wavenumber * wavenumber


def coulomb(first_row, row_count):
    squared = (
        wave_square(NZ, 0, NZ)[:, None, None]
        + wave_square(row_count, first_row, NY)[None, :, None]
        + wave_square(NX, 0, NX)[None, None, :]
    )
    safe_square = jnp.where(squared > 0.0, squared, 1.0)
    return jnp.where(squared > 0.0, 4.0 * math.pi / safe_square, 0.0)


def fourier_table(length, inverse):
    position = jnp.arange(length, dtype=jnp.int32)
    phase_turns = position[:, None] * position[None, :] % length
    phase_angle = 2.0 * math.pi / length * phase_turns.astype(jnp.float32)
    cosine = jnp.cos(phase_angle)
    sine_part = jnp.sin(phase_angle)
    norm_factor = 1.0
    if inverse:
        sine_part = -sine_part
        norm_factor = 1.0 / length
    return norm_factor * jnp.stack(
        [jnp.stack([cosine, -sine_part]), jnp.stack([sine_part, cosine])]
    )


def solve_pairs(packed, kernel_slab):
    spectrum = jnp.einsum(
        "pczyx,cdxk->dpzyk", packed, fourier_table(NX, False), precision=HIGHEST_PRECISION
    )
    spectrum = jnp.einsum(
        "cpzyx,cdyk->dpzkx", spectrum, fourier_table(NY, False), precision=HIGHEST_PRECISION
    )
    forward_z = fourier_table(NZ, False)
    inverse_z = fourier_table(NZ, True)
    screened = (
        jnp.einsum(
            "cpzyx,cdzk->dpkyx",
            lax.all_to_all(spectrum, "grid", split_axis=3, concat_axis=2, tiled=True),
            forward_z,
            precision=HIGHEST_PRECISION,
        )
        * kernel_slab
    )
    screened = jnp.einsum("cpzyx,cdzk->dpkyx", screened, inverse_z, precision=HIGHEST_PRECISION)
    planes = lax.all_to_all(screened, "grid", split_axis=2, concat_axis=3, tiled=True)
    planes = jnp.einsum(
        "cpzyx,cdyk->dpzkx", planes, fourier_table(NY, True), precision=HIGHEST_PRECISION
    )
    return jnp.einsum(
        "cpzyx,cdxk->pdzyk", planes, fourier_table(NX, True), precision=HIGHEST_PRECISION
    )


def pair_terms(owned, visitors, kernel_slab):
    count_vis = visitors.shape[0]
    count_own = owned.shape[0]
    density = owned[None] * visitors[:, None]
    packed = density.reshape((count_vis * count_own // 2, 2) + owned.shape[1:])
    potential = solve_pairs(packed, kernel_slab).reshape(density.shape)
    own_part = jnp.sum(potential * visitors[:, None], axis=0)
    partner = jnp.sum(potential * owned[None], axis=1)
    return (own_part, partner)


def arrive(travel):
    return passed_along(travel, "band", 1)


def send_back(partner):
    return passed_along(partner, "band", -1)


def body(own_bands, travel_bands):
    rows_local = NY // lax.axis_size("grid")
    kernel_slab = coulomb(lax.axis_index("grid") * rows_local, rows_local)
    count_vis = travel_bands.shape[0]
    visitors = arrive(travel_bands)
    own_total = jnp.zeros_like(own_bands)
    held_parts = []
    for visit_index in range(count_vis):
        own_part, partner = pair_terms(
            own_bands, visitors[visit_index : visit_index + 1], kernel_slab
        )
        own_total = own_total + own_part
        held_parts.append(partner)
    partner_total = send_back(jnp.concatenate(held_parts, axis=0))
    return (-FRACTION * own_total, -FRACTION * partner_total)


def solution(mesh):
    in_specs = (P("band", "grid", None, None), P("band", "grid", None, None))
    out_specs = (P("band", "grid", None, None), P("band", "grid", None, None))
    return jax.shard_map(body, mesh=mesh, in_specs=in_specs, out_specs=out_specs, check_vma=False)
```

profile of v0, /device:TPU:1, one launch (start us, length us, event | category | flops | bytes accessed | tf_op | source)
XLA Modules:
  0.0 394.6 jit_solution(8856998799125972145)
XLA Ops:
  0.6 2.5 collective-permute-start
  3.8 51.5 %collective-permute-done = f32[4,8,128,128]{3,2,1,0:T(8,128)S(1)} collective-permute-done((f32[4,8,128,128]{3,2,1,0:T(8,128)}, f32[4,8,128,128]{3,2,1,0:T(8,128)S(1)}, u32[]{:S(2)}, u32[]{:S(2)}) %collective-permute-start) | collective-permute-done | bytes 2097184 | tf_op jit(solution)/shard_map/ppermute | solution.py:20
  55.5 3.1 broadcast_multiply_fusion.4
  62.6 2.5 copy.106
  65.1 5.9 %all-to-all-start.4 = ((f32[2,2,8,128,128]{4,2,1,0,3:T(8,128)}), f32[2,2,8,128,128]{4,2,1,0,3:T(8,128)S(1)}, u32[]{:S(2)}, u32[]{:S(2)}) async-start(f32[2,2,8,128,128]{4,2,1,0,3:T(8,128)} %copy.106), calls=%async_computation.4 | async-start | bytes 4194304 | tf_op jit(solution)/shard_map/all_to_all | solution.py:67
  71.0 3.5 fusion.58
  76.5 2.5 copy.78
  79.1 19.5 %all-to-all-done.4 = f32[2,2,8,128,128]{4,2,1,0,3:T(8,128)S(1)} async-done(((f32[2,2,8,128,128]{4,2,1,0,3:T(8,128)}), f32[2,2,8,128,128]{4,2,1,0,3:T(8,128)S(1)}, u32[]{:S(2)}, u32[]{:S(2)}) %all-to-all-start.4) | async-done | bytes 2097184 | tf_op jit(solution)/shard_map/all_to_all | solution.py:67
  99.9 4.7 %all-to-all-start = ((f32[2,2,8,128,128]{4,2,1,0,3:T(8,128)}), f32[2,2,8,128,128]{4,2,1,0,3:T(8,128)S(1)}, u32[]{:S(2)}, u32[]{:S(2)}) async-start(f32[2,2,8,128,128]{4,2,1,0,3:T(8,128)} %copy.78), calls=%async_computation | async-start | bytes 4194304 | tf_op jit(solution)/shard_map/all_to_all | solution.py:67
  104.5 3.5 fusion.52
  110.0 2.5 copy.92
  112.6 19.6 %all-to-all-done = f32[2,2,8,128,128]{4,2,1,0,3:T(8,128)S(1)} async-done(((f32[2,2,8,128,128]{4,2,1,0,3:T(8,128)}), f32[2,2,8,128,128]{4,2,1,0,3:T(8,128)S(1)}, u32[]{:S(2)}, u32[]{:S(2)}) %all-to-all-start) | async-done | bytes 2097184 | tf_op jit(solution)/shard_map/all_to_all | solution.py:67
  133.4 5.0 %all-to-all-start.2 = ((f32[2,2,8,128,128]{4,2,1,0,3:T(8,128)}), f32[2,2,8,128,128]{4,2,1,0,3:T(8,128)S(1)}, u32[]{:S(2)}, u32[]{:S(2)}) async-start(f32[2,2,8,128,128]{4,2,1,0,3:T(8,128)} %copy.92), calls=%async_computation.2 | async-start | bytes 4194304 | tf_op jit(solution)/shard_map/all_to_all | solution.py:67
  138.4 3.5 fusion.38
  143.9 2.5 copy.120
  146.5 19.5 %all-to-all-done.2 = f32[2,2,8,128,128]{4,2,1,0,3:T(8,128)S(1)} async-done(((f32[2,2,8,128,128]{4,2,1,0,3:T(8,128)}), f32[2,2,8,128,128]{4,2,1,0,3:T(8,128)S(1)}, u32[]{:S(2)}, u32[]{:S(2)}) %all-to-all-start.2) | async-done | bytes 2097184 | tf_op jit(solution)/shard_map/all_to_all | solution.py:67
  167.2 4.7 %all-to-all-start.6 = ((f32[2,2,8,128,128]{4,2,1,0,3:T(8,128)}), f32[2,2,8,128,128]{4,2,1,0,3:T(8,128)S(1)}, u32[]{:S(2)}, u32[]{:S(2)}) async-start(f32[2,2,8,128,128]{4,2,1,0,3:T(8,128)} %copy.120), calls=%async_computation.6 | async-start | bytes 4194304 | tf_op jit(solution)/shard_map/all_to_all | solution.py:67
  172.2 2.8 copy.108
  175.0 2.1 fusion.43
  179.1 2.5 copy.111
  181.7 17.8 %all-to-all-done.6 = f32[2,2,8,128,128]{4,2,1,0,3:T(8,128)S(1)} async-done(((f32[2,2,8,128,128]{4,2,1,0,3:T(8,128)}), f32[2,2,8,128,128]{4,2,1,0,3:T(8,128)S(1)}, u32[]{:S(2)}, u32[]{:S(2)}) %all-to-all-start.6) | async-done | bytes 2097184 | tf_op jit(solution)/shard_map/all_to_all | solution.py:67
  199.5 5.3 %all-to-all-start.5 = ((f32[2,2,128,8,128]{4,3,1,0,2:T(8,128)}), f32[2,2,128,8,128]{4,3,1,0,2:T(8,128)}, u32[]{:S(2)}, u32[]{:S(2)}) async-start(f32[2,2,128,8,128]{4,3,1,0,2:T(8,128)} %copy.111), calls=%async_computation.5 | async-start | bytes 4194304 | tf_op jit(solution)/shard_map/all_to_all | solution.py:74
  204.8 2.8 copy.80
  207.6 2.1 fusion.56
  211.7 2.5 copy.83
  214.3 17.8 %all-to-all-done.5 = f32[2,2,128,8,128]{4,3,1,0,2:T(8,128)} async-done(((f32[2,2,128,8,128]{4,3,1,0,2:T(8,128)}), f32[2,2,128,8,128]{4,3,1,0,2:T(8,128)}, u32[]{:S(2)}, u32[]{:S(2)}) %all-to-all-start.5) | async-done | bytes 2097184 | tf_op jit(solution)/shard_map/all_to_all | solution.py:74
  232.1 5.4 %all-to-all-start.1 = ((f32[2,2,128,8,128]{4,3,1,0,2:T(8,128)}), f32[2,2,128,8,128]{4,3,1,0,2:T(8,128)}, u32[]{:S(2)}, u32[]{:S(2)}) async-start(f32[2,2,128,8,128]{4,3,1,0,2:T(8,128)} %copy.83), calls=%async_computation.1 | async-start | bytes 4194304 | tf_op jit(solution)/shard_map/all_to_all | solution.py:74
  237.5 2.8 copy.94
  240.3 2.1 fusion.50
  244.4 2.5 copy.97
  246.9 18.0 %all-to-all-done.1 = f32[2,2,128,8,128]{4,3,1,0,2:T(8,128)} async-done(((f32[2,2,128,8,128]{4,3,1,0,2:T(8,128)}), f32[2,2,128,8,128]{4,3,1,0,2:T(8,128)}, u32[]{:S(2)}, u32[]{:S(2)}) %all-to-all-start.1) | async-done | bytes 2097184 | tf_op jit(solution)/shard_map/all_to_all | solution.py:74
  264.9 5.1 %all-to-all-start.3 = ((f32[2,2,128,8,128]{4,3,1,0,2:T(8,128)}), f32[2,2,128,8,128]{4,3,1,0,2:T(8,128)}, u32[]{:S(2)}, u32[]{:S(2)}) async-start(f32[2,2,128,8,128]{4,3,1,0,2:T(8,128)} %copy.97), calls=%async_computation.3 | async-start | bytes 4194304 | tf_op jit(solution)/shard_map/all_to_all | solution.py:74
  271.3 2.1 fusion.36
  275.4 2.6 copy.125
  278.0 19.4 %all-to-all-done.3 = f32[2,2,128,8,128]{4,3,1,0,2:T(8,128)} async-done(((f32[2,2,128,8,128]{4,3,1,0,2:T(8,128)}), f32[2,2,128,8,128]{4,3,1,0,2:T(8,128)}, u32[]{:S(2)}, u32[]{:S(2)}) %all-to-all-start.3) | async-done | bytes 2097184 | tf_op jit(solution)/shard_map/all_to_all | solution.py:74
  297.4 5.3 %all-to-all-start.7 = ((f32[2,2,128,8,128]{4,3,1,0,2:T(8,128)}), f32[2,2,128,8,128]{4,3,1,0,2:T(8,128)S(1)}, u32[]{:S(2)}, u32[]{:S(2)}) async-start(f32[2,2,128,8,128]{4,3,1,0,2:T(8,128)} %copy.125), calls=%async_computation.7 | async-start | bytes 4194304 | tf_op jit(solution)/shard_map/all_to_all | solution.py:74
  302.7 3.5 fusion.10
  306.2 3.3 fusion.90
  309.5 2.9 copy.117
  312.4 3.5 fusion.14
  315.9 3.3 fusion.84
  319.2 2.9 copy.89
  322.1 3.5 fusion.12
  325.6 3.3 fusion.87
  328.8 3.2 copy.103
  337.8 7.5 %fusion.54 = (f32[8,128,128]{2,1,0:T(8,128)S(1)}, f32[8,128,128]{2,1,0:T(8,128)S(1)}, f32[8,128,128]{2,1,0:T(8,128)S(1)}, f32[8,128,128]{2,1,0:T(8,128)S(1)}, f32[4,8,128,128]{3,2,1,0:T(8,128)}) fusion(f32[4,8,128,128]{3,2,1,0:T(8,128)} %param.2, f32[2,2,8,128,128]{4,3,2,1,0:T(8,128)} %copy.89, f32[2,2,8,128,128]{4,3,2,1,0:T(8,128)} %copy.103, ...), kind=kLoop, calls=%fused_computation.69 | loop fusion | flops 7864320 | bytes 16777216 | tf_op jit(solution)/shard_map/reduce_sum | solution.py:90
  345.4 2.1 collective-permute-start.1
  347.6 45.1 %collective-permute-done.1 = f32[4,8,128,128]{3,2,1,0:T(8,128)S(1)} collective-permute-done((f32[4,8,128,128]{3,2,1,0:T(8,128)S(1)}, f32[4,8,128,128]{3,2,1,0:T(8,128)S(1)}, u32[]{:S(2)}, u32[]{:S(2)}) %collective-permute-start.1) | collective-permute-done | bytes 2097184 | tf_op jit(solution)/shard_map/ppermute | solution.py:20
  (44 shorter events, 31.2 us)
Async XLA Ops:
  0.6 54.6 %collective-permute-start = (f32[4,8,128,128]{3,2,1,0:T(8,128)}, f32[4,8,128,128]{3,2,1,0:T(8,128)S(1)}, u32[]{:S(2)}, u32[]{:S(2)}) collective-permute-start(f32[4,8,128,128]{3,2,1,0:T(8,128)} %param.3), channel_id=1, source_target_pairs={{240,0},{0,16},{16,32},{32,48},{48,64},{64,80},{80,96},{96,112},{1... | collective-permute-start | bytes 6291464 | tf_op jit(solution)/shard_map/ppermute | solution.py:20
  3.7 51.7 %copy-start.3 = (f32[4,8,128,128]{3,2,1,0:T(8,128)S(1)}, f32[4,8,128,128]{3,2,1,0:T(8,128)}, u32[]{:S(2)}) copy-start(f32[4,8,128,128]{3,2,1,0:T(8,128)} %param.2) | copy-start | bytes 6291460
  55.4 3.2 copy-start.4
  55.4 3.2 copy-start.6
  55.4 3.2 copy-start.8
  55.5 3.2 copy-start.9
  65.1 33.4 %all-to-all-start.4 = ((f32[2,2,8,128,128]{4,2,1,0,3:T(8,128)}), f32[2,2,8,128,128]{4,2,1,0,3:T(8,128)S(1)}, u32[]{:S(2)}, u32[]{:S(2)}) async-start(f32[2,2,8,128,128]{4,2,1,0,3:T(8,128)} %copy.106), calls=%async_computation.4 | async-start | bytes 4194304 | tf_op jit(solution)/shard_map/all_to_all | solution.py:67
  98.5 1.3 copy-start.2
  99.9 32.3 %all-to-all-start = ((f32[2,2,8,128,128]{4,2,1,0,3:T(8,128)}), f32[2,2,8,128,128]{4,2,1,0,3:T(8,128)S(1)}, u32[]{:S(2)}, u32[]{:S(2)}) async-start(f32[2,2,8,128,128]{4,2,1,0,3:T(8,128)} %copy.78), calls=%async_computation | async-start | bytes 4194304 | tf_op jit(solution)/shard_map/all_to_all | solution.py:67
  132.1 1.3 copy-start.1
  133.4 32.5 %all-to-all-start.2 = ((f32[2,2,8,128,128]{4,2,1,0,3:T(8,128)}), f32[2,2,8,128,128]{4,2,1,0,3:T(8,128)S(1)}, u32[]{:S(2)}, u32[]{:S(2)}) async-start(f32[2,2,8,128,128]{4,2,1,0,3:T(8,128)} %copy.92), calls=%async_computation.2 | async-start | bytes 4194304 | tf_op jit(solution)/shard_map/all_to_all | solution.py:67
  165.9 1.3 copy-start
  167.2 32.3 %all-to-all-start.6 = ((f32[2,2,8,128,128]{4,2,1,0,3:T(8,128)}), f32[2,2,8,128,128]{4,2,1,0,3:T(8,128)S(1)}, u32[]{:S(2)}, u32[]{:S(2)}) async-start(f32[2,2,8,128,128]{4,2,1,0,3:T(8,128)} %copy.120), calls=%async_computation.6 | async-start | bytes 4194304 | tf_op jit(solution)/shard_map/all_to_all | solution.py:67
  199.5 32.6 %all-to-all-start.5 = ((f32[2,2,128,8,128]{4,3,1,0,2:T(8,128)}), f32[2,2,128,8,128]{4,3,1,0,2:T(8,128)}, u32[]{:S(2)}, u32[]{:S(2)}) async-start(f32[2,2,128,8,128]{4,3,1,0,2:T(8,128)} %copy.111), calls=%async_computation.5 | async-start | bytes 4194304 | tf_op jit(solution)/shard_map/all_to_all | solution.py:74
  232.1 32.8 %all-to-all-start.1 = ((f32[2,2,128,8,128]{4,3,1,0,2:T(8,128)}), f32[2,2,128,8,128]{4,3,1,0,2:T(8,128)}, u32[]{:S(2)}, u32[]{:S(2)}) async-start(f32[2,2,128,8,128]{4,3,1,0,2:T(8,128)} %copy.83), calls=%async_computation.1 | async-start | bytes 4194304 | tf_op jit(solution)/shard_map/all_to_all | solution.py:74
  264.9 32.4 %all-to-all-start.3 = ((f32[2,2,128,8,128]{4,3,1,0,2:T(8,128)}), f32[2,2,128,8,128]{4,3,1,0,2:T(8,128)}, u32[]{:S(2)}, u32[]{:S(2)}) async-start(f32[2,2,128,8,128]{4,3,1,0,2:T(8,128)} %copy.97), calls=%async_computation.3 | async-start | bytes 4194304 | tf_op jit(solution)/shard_map/all_to_all | solution.py:74
  297.4 34.7 %all-to-all-start.7 = ((f32[2,2,128,8,128]{4,3,1,0,2:T(8,128)}), f32[2,2,128,8,128]{4,3,1,0,2:T(8,128)S(1)}, u32[]{:S(2)}, u32[]{:S(2)}) async-start(f32[2,2,128,8,128]{4,3,1,0,2:T(8,128)} %copy.125), calls=%async_computation.7 | async-start | bytes 4194304 | tf_op jit(solution)/shard_map/all_to_all | solution.py:74
  335.9 1.8 copy-start.5
  335.9 1.8 copy-start.7
  345.4 47.3 %collective-permute-start.1 = (f32[4,8,128,128]{3,2,1,0:T(8,128)S(1)}, f32[4,8,128,128]{3,2,1,0:T(8,128)S(1)}, u32[]{:S(2)}, u32[]{:S(2)}) collective-permute-start(f32[4,8,128,128]{3,2,1,0:T(8,128)S(1)} %pad_maximum_fusion), channel_id=1, source_target_pairs={{16,0},{32,16},{48,32},{64,48},{80,64},{96,80},{112,96},{128,112},... | collective-permute-start | bytes 6291464 | tf_op jit(solution)/shard_map/ppermute | solution.py:20
where the time goes:
time: 401 us; the launch traced here: 395 us
  waiting for transfers between devices  228 us (57%)
  matrix products  60.9 us (15%)
  starting transfers between devices  46.1 us (11%)
  local copies, waits for them, and re-layouts  44.9 us (11%)
  other arithmetic  13.1 us (3%)
    ppermute x2, waiting for transfers between devices, passed_along(): return lax.ppermute(block, axis, route)  96.6 us
    all_to_all x4, waiting for transfers between devices, solve_pairs(): lax.all_to_all(spectrum, 'grid', split_axis=3, concat_axis=2, tiled=True)  76.3 us
    all_to_all x4, waiting for transfers between devices, solve_pairs(): lax.all_to_all(screened, 'grid', split_axis=2, concat_axis=3, tiled=True)  55.2 us
    all_to_all x4, starting transfers between devices, solve_pairs(): lax.all_to_all(screened, 'grid', split_axis=2, concat_axis=3, tiled=True)  21.1 us
    all_to_all x4, starting transfers between devices, solve_pairs(): lax.all_to_all(spectrum, 'grid', split_axis=3, concat_axis=2, tiled=True)  20.2 us
    dot_general x4, matrix products, solve_pairs(): jnp.einsum('pczyx,cdxk->dpzyk', packed, fourier_table(NX, False), precisi...  12.5 us
    dot_general x4, matrix products, solve_pairs(): jnp.einsum('cpzyx,cdyk->dpzkx', planes, fourier_table(NY, True), precisio...  12.5 us
    dot_general x4, matrix products, solve_pairs(): jnp.einsum('cpzyx,cdxk->pdzyk', planes, fourier_table(NX, True), precisio...  11.7 us
  transfers between devices with their start and end apart: 10, of which 9 were waited for; matrix products, arithmetic and copies ran while one was open for 23% of the time, Pallas kernels for 0%

commit v1 on v0

v1 whole, which is shorter than its diff:
```python
import functools
import math

import jax
import jax.numpy as jnp
import ml_dtypes
import numpy as np
from jax import lax
from jax.experimental import pallas as pl
from jax.experimental.pallas import tpu as pltpu
from jax.sharding import PartitionSpec as P

N = 128
FRACTION = 0.25
ROW = 8
KYS = N // ROW
LOCAL = 8
VIS = 4
PAIRED = 2
BLOCK = LOCAL * KYS
PAIR_ROWS = 2 * ROW * BLOCK
STEPS = ((2, 0), (2, 1), (1, 0), (3, 0), (1, 1), (3, 1), (0, 1))
F32 = jnp.float32
BF16 = jnp.bfloat16
MESH = pl.DeviceIdType.MESH


def real_basis():
    n = np.arange(N)
    rows = []
    for m in range(N):
        if m <= N // 2:
            row = np.cos(2.0 * np.pi * ((m * n) % N) / N)
        else:
            row = np.sin(2.0 * np.pi * (((N - m) * n) % N) / N)
        scale = 1.0 / N if m in (0, N // 2) else 2.0 / N
        rows.append(np.sqrt(scale) * row)
    return np.stack(rows)


def high_low(table):
    high = table.astype(np.float32).astype(ml_dtypes.bfloat16)
    low = (table - high.astype(np.float64)).astype(np.float32).astype(ml_dtypes.bfloat16)
    return high, low


def tables():
    basis = real_basis()
    high, low = high_low(basis)
    high_t, low_t = high.T, low.T
    from_left = np.block([[high, high], [low, low]])
    from_left_inverse = np.block([[high_t, high_t], [low_t, low_t]])
    from_right = np.block([[high_t, low_t], [high_t, low_t]])
    from_right_inverse = np.block([[high, low], [high, low]])
    return [from_left, from_left_inverse, from_right, from_right_inverse]


def halves(value, axis):
    high = value.astype(BF16)
    low = (value - high.astype(F32)).astype(BF16)
    return jnp.concatenate([high, low], axis=axis)


def along_rows(table, value):
    both = jnp.dot(table, halves(value, 0), preferred_element_type=F32)
    return both[:N] + both[N:]


def along_lanes(value, table):
    both = jnp.dot(halves(value, 1), table, preferred_element_type=F32)
    return both[:, :N] + both[:, N:]


def wave_square(position):
    position = lax.rem(position + N // 2, N) - N // 2
    number = 2.0 * math.pi / N * position.astype(F32)
    return number * number


def kernel(
    own, travel, lt_ref, lti_ref, wx_ref, wxi_ref, own_out, held_out,
    ownb, visb, send, recv, back, own_sum, held, held_part, coulomb,
    load_sem, exch_send, exch_recv, vis_send, vis_recv, relay_send, relay_recv,
    fwd_send, fwd_recv, bwd_send, bwd_recv,
    part_send, part_recv, out_send, out_recv, ret_send, ret_recv, store_sem,
):
    band = lax.axis_index("band")
    groups = lax.axis_size("band")
    grid = lax.axis_index("grid")
    mine = grid // ROW
    other = 1 - mine
    place = grid % ROW
    x, core = place // 2, place % 2
    partner = {"grid": other * ROW + place}
    ahead = {"band": (band + 1) % groups}
    behind = {"band": (band + groups - 1) % groups}
    places = [((x + dx) % 4) * 2 + (core + dc) % 2 for dx, dc in STEPS]
    peers = [{"grid": mine * ROW + p} for p in places]

    def remote(src, dst, send_sem, recv_sem, device):
        return pltpu.make_async_remote_copy(
            src_ref=src, dst_ref=dst, send_sem=send_sem, recv_sem=recv_sem,
            device_id=device, device_id_type=MESH,
        )

    for i in range(PAIRED):
        pltpu.make_async_copy(own.at[2 * mine + i], ownb.at[i, mine], load_sem.at[i]).start()

    barrier = pltpu.get_barrier_semaphore()
    for device in [ahead, behind, partner] + peers:
        pl.semaphore_signal(barrier, inc=1, device_id=device, device_id_type=MESH)
    pl.semaphore_wait(barrier, 3 + len(peers))

    def visitor(j, q):
        return remote(
            travel.at[j, pl.ds(2 * q, 2)], visb.at[j, mine, pl.ds(2 * q, 2)],
            vis_send.at[j, q], vis_recv.at[j, q], ahead,
        )

    def relay(j, q, half):
        return remote(
            visb.at[j, half, pl.ds(2 * q, 2)], visb.at[j, half, pl.ds(2 * q, 2)],
            relay_send.at[j, q], relay_recv.at[j, q], partner,
        )

    def exchange(i, half, index):
        return remote(own.at[index], ownb.at[i, half], exch_send.at[i], exch_recv.at[i], partner)

    for j in range(VIS):
        for q in range(4):
            visitor(j, q).start()
        if j == 0:
            for i in range(PAIRED):
                exchange(i, mine, 2 * other + i).start()

    kz = lax.broadcasted_iota(jnp.int32, (N, 2 * N), 0)
    lane = lax.broadcasted_iota(jnp.int32, (N, 2 * N), 1)
    kx_square = wave_square(lax.rem(lane, N))
    kz_square = wave_square(kz)

    def fill(kp, carry):
        ky = place * KYS + 2 * kp + lane // N
        squared = kz_square + wave_square(ky) + kx_square
        safe = jnp.where(squared > 0.0, squared, 1.0)
        value = jnp.where(squared > 0.0, 4.0 * math.pi / safe, 0.0)
        coulomb[kp] = -FRACTION * value
        return carry

    lax.fori_loop(0, KYS // 2, fill, 0)

    def base(j, i, half, p):
        return ((j * PAIRED + i) * 2 + half) * ROW * BLOCK + p * BLOCK

    def rows(ref, start, count):
        return ref.at[pl.ds(pl.multiple_of(start, KYS), count)]

    def forward(j, half, own_half):
        def piece(q, carry):
            if own_half:
                visitor(j, q).wait_recv()
                relay(j, q, mine).start()
            else:
                relay(j, q, other).wait_recv()
            planes = pl.ds(2 * q, 2)
            vis = visb[j, half, planes].reshape(2 * N, N)
            for i in range(PAIRED):
                density = ownb[i, half, planes].reshape(2 * N, N) * vis
                wave = along_lanes(density, wx_ref[...])
                wave = jnp.concatenate([wave[:N], wave[N:]], axis=1)
                wave = along_rows(lt_ref[...], wave)
                for p in range(ROW):
                    for z in range(2):
                        start = base(j, i, half, p) + (2 * q + z) * KYS
                        send[pl.ds(pl.multiple_of(start, KYS), KYS), :] = wave[
                            p * KYS : (p + 1) * KYS, z * N : (z + 1) * N
                        ]
                start = pl.multiple_of(base(j, i, half, place) + 2 * q * KYS, KYS)
                recv[pl.ds(start, 2 * KYS), :] = send[pl.ds(start, 2 * KYS), :]
            for i in range(PAIRED):
                for p, peer in zip(places, peers):
                    remote(
                        rows(send, base(j, i, half, p) + 2 * q * KYS, 2 * KYS),
                        rows(recv, base(j, i, half, place) + 2 * q * KYS, 2 * KYS),
                        fwd_send, fwd_recv.at[j, half], peer,
                    ).start()
            return carry

        lax.fori_loop(0, 4, piece, 0)

    def screen(j):
        for half in (mine, other):
            whole = rows(recv, 0, (ROW - 1) * PAIRED * BLOCK)
            remote(whole, whole, fwd_send, fwd_recv.at[j, half], partner).wait_recv()

        def columns(step, carry):
            i, kp = step // (KYS // 2), step % (KYS // 2)
            start = (j * PAIRED + i) * PAIR_ROWS + 2 * kp
            first = pl.ds(start, N, stride=KYS)
            second = pl.ds(start + 1, N, stride=KYS)
            wave = jnp.concatenate([recv[first, :], recv[second, :]], axis=1)
            wave = along_rows(lt_ref[...], wave) * coulomb[kp]
            wave = along_rows(lti_ref[...], wave)
            recv[first, :] = wave[:, :N]
            recv[second, :] = wave[:, N:]
            return carry

        lax.fori_loop(0, PAIRED * KYS // 2, columns, 0)
        for i in range(PAIRED):
            for half in range(2):
                start = pl.multiple_of(base(j, i, half, place), KYS)
                back[pl.ds(start, BLOCK), :] = recv[pl.ds(start, BLOCK), :]
        for half in (other, mine):
            for zq in range(2):
                for i in range(PAIRED):
                    for p, peer in zip(places, peers):
                        remote(
                            rows(recv, base(j, i, half, p) + zq * (BLOCK // 2), BLOCK // 2),
                            rows(back, base(j, i, half, place) + zq * (BLOCK // 2), BLOCK // 2),
                            bwd_send, bwd_recv.at[j, half, zq], peer,
                        ).start()

    def inverse(j, half, zq):
        whole = rows(back, 0, (ROW - 1) * PAIRED * (BLOCK // 2))
        remote(whole, whole, bwd_send, bwd_recv.at[j, half, zq], partner).wait_recv()

        def planes_of(step, carry):
            zp, i = step // PAIRED, step % PAIRED
            z = 4 * zq + 2 * zp
            sides = []
            for k in range(2):
                parts = []
                for p in range(ROW):
                    start = base(j, i, half, p) + (z + k) * KYS
                    parts.append(back[pl.ds(pl.multiple_of(start, KYS), KYS), :])
                sides.append(jnp.concatenate(parts, axis=0))
            wave = along_rows(lti_ref[...], jnp.concatenate(sides, axis=1))
            wave = jnp.concatenate([wave[:, :N], wave[:, N:]], axis=0)
            potential = along_lanes(wave, wxi_ref[...]).reshape(2, N, N)
            planes = pl.ds(z, 2)
            own_part = potential * visb[j, half, planes]
            if j > 0:
                own_part = own_part + own_sum[i, half, planes]
            own_sum[i, half, planes] = own_part
            held_term = potential * ownb[i, half, planes]

            @pl.when(i == 0)
            def _():
                held[j, half, planes] = held_term

            @pl.when(i > 0)
            def _():
                held[j, half, planes] = held[j, half, planes] + held_term

            return carry

        lax.fori_loop(0, 2 * PAIRED, planes_of, 0)

    def partial(j, zq):
        planes = pl.ds(4 * zq, 4)
        return remote(
            held.at[j, other, planes], held_part.at[j, planes],
            part_send.at[j, zq], part_recv.at[j, zq], partner,
        )

    def outgoing(j, zq):
        planes = pl.ds(4 * zq, 4)
        return remote(
            held.at[j, mine, planes], held_out.at[j, planes],
            out_send.at[j, zq], out_recv.at[j, zq], behind,
        )

    def returned(i, zq):
        planes = pl.ds(4 * zq, 4)
        return remote(
            own_sum.at[i, other, planes], own_out.at[2 * mine + i, planes],
            ret_send.at[i, zq], ret_recv.at[i, zq], partner,
        )

    def stored(i, zq):
        planes = pl.ds(4 * zq, 4)
        return pltpu.make_async_copy(
            own_sum.at[i, mine, planes], own_out.at[2 * mine + i, planes], store_sem.at[i, zq]
        )

    def back_part(j):
        for zq in range(2):
            inverse(j, other, zq)
            partial(j, zq).start()
            if j == VIS - 1:
                for i in range(PAIRED):
                    returned(i, zq).start()
        for zq in range(2):
            inverse(j, mine, zq)
            if j == VIS - 1:
                for i in range(PAIRED):
                    stored(i, zq).start()
                settle(j, zq)

    def settle(j, zq):
        partial(j, zq).wait_recv()
        planes = pl.ds(4 * zq, 4)
        held[j, mine, planes] = held[j, mine, planes] + held_part[j, planes]
        outgoing(j, zq).start()

    def settle_all(j):
        for zq in range(2):
            settle(j, zq)

    for i in range(PAIRED):
        pltpu.make_async_copy(own.at[2 * mine + i], ownb.at[i, mine], load_sem.at[i]).wait()
    forward(0, mine, True)
    forward(1, mine, True)
    forward(2, mine, True)
    for i in range(PAIRED):
        exchange(i, other, 2 * mine + i).wait_recv()
    forward(0, other, False)
    forward(3, mine, True)
    screen(0)
    forward(1, other, False)
    forward(2, other, False)
    screen(1)
    back_part(0)
    forward(3, other, False)
    screen(2)
    settle_all(0)
    back_part(1)
    screen(3)
    settle_all(1)
    back_part(2)
    settle_all(2)
    back_part(3)

    for j in range(VIS):
        for q in range(4):
            visitor(j, q).wait_send()
            relay(j, q, mine).wait_send()
    for i in range(PAIRED):
        exchange(i, mine, 2 * other + i).wait_send()
    sent = rows(send, 0, (ROW - 1) * PAIRED * 2 * VIS * BLOCK)
    remote(sent, sent, fwd_send, fwd_recv.at[0, 0], partner).wait_send()
    remote(sent, sent, bwd_send, fwd_recv.at[0, 0], partner).wait_send()
    for zq in range(2):
        for j in range(VIS):
            partial(j, zq).wait_send()
            outgoing(j, zq).wait()
        for i in range(PAIRED):
            returned(i, zq).wait()
            stored(i, zq).wait()


def body(own_bands, travel_bands):
    table_list = [jnp.asarray(t) for t in tables()]
    whole = 4 * PAIR_ROWS * PAIRED
    dma = pltpu.SemaphoreType.DMA
    any_space = pl.BlockSpec(memory_space=pl.ANY)
    vmem = pl.BlockSpec(memory_space=pltpu.VMEM)
    return pl.pallas_call(
        kernel,
        out_shape=[
            jax.ShapeDtypeStruct(own_bands.shape, F32),
            jax.ShapeDtypeStruct(travel_bands.shape, F32),
        ],
        in_specs=[any_space, any_space] + [vmem] * 4,
        out_specs=[any_space, any_space],
        scratch_shapes=[
            pltpu.VMEM((PAIRED, 2, LOCAL, N, N), F32),
            pltpu.VMEM((VIS, 2, LOCAL, N, N), F32),
            pltpu.VMEM((whole, N), F32),
            pltpu.VMEM((whole, N), F32),
            pltpu.VMEM((whole, N), F32),
            pltpu.VMEM((PAIRED, 2, LOCAL, N, N), F32),
            pltpu.VMEM((VIS, 2, LOCAL, N, N), F32),
            pltpu.VMEM((VIS, LOCAL, N, N), F32),
            pltpu.VMEM((KYS // 2, N, 2 * N), F32),
            dma((PAIRED,)),
            dma((PAIRED,)),
            dma((PAIRED,)),
            dma((VIS, 4)),
            dma((VIS, 4)),
            dma((VIS, 4)),
            dma((VIS, 4)),
            dma,
            dma((VIS, 2)),
            dma,
            dma((VIS, 2, 2)),
            dma((VIS, 2)),
            dma((VIS, 2)),
            dma((VIS, 2)),
            dma((VIS, 2)),
            dma((PAIRED, 2)),
            dma((PAIRED, 2)),
            dma((PAIRED, 2)),
        ],
        compiler_params=pltpu.CompilerParams(
            collective_id=0, has_side_effects=True, vmem_limit_bytes=60 * 2**20
        ),
        name="exchange_terms",
    )(own_bands, travel_bands, *table_list)


def solution(mesh):
    in_specs = (P("band", "grid", None, None), P("band", "grid", None, None))
    out_specs = (P("band", "grid", None, None), P("band", "grid", None, None))
    return jax.shard_map(body, mesh=mesh, in_specs=in_specs, out_specs=out_specs, check_vma=False)
```

time: 401 us -> 259 us (0.65); the launches traced: 395 us -> 259 us
  Pallas kernels: 0 us -> 254 us
  waiting for transfers between devices: 228 us -> 0 us
  matrix products: 60.9 us -> 0 us
  starting transfers between devices: 46.1 us -> 0 us
  local copies, waits for them, and re-layouts: 44.9 us -> 4.61 us
  other arithmetic: 13.1 us -> 0 us
    pallas_call x0 -> x1, Pallas kernels: none -> 254 us  [body(): pl.pallas_call(kernel, out_shape=[jax.ShapeDtypeStruct(own_bands.shape, F...]
    all_to_all x8 -> x0, waiting for transfers between devices: 132 us -> none  [the longest x4 76.3 us: solve_pairs(): lax.all_to_all(spectrum, 'grid', split_axis=3, concat_axis=2, tiled=True)]
    ppermute x2 -> x0, waiting for transfers between devices: 96.6 us -> none  [passed_along(): return lax.ppermute(block, axis, route)]
    dot_general x24 -> x0, matrix products: 60.9 us -> none  [the longest x4 12.5 us: solve_pairs(): jnp.einsum('pczyx,cdxk->dpzyk', packed, fourier_table(NX, False), precisi...]
    all_to_all x8 -> x0, starting transfers between devices: 41.4 us -> none  [the longest x4 21.1 us: solve_pairs(): lax.all_to_all(screened, 'grid', split_axis=2, concat_axis=3, tiled=True)]
    transpose x12 -> x0, local copies, waits for them, and re-layouts: 31.1 us -> none  [the longest x4 10.8 us: solve_pairs(): jnp.einsum('cpzyx,cdxk->pdzyk', planes, fourier_table(NX, True), precisio...]
    all_to_all x4 -> x0, local copies, waits for them, and re-layouts: 9.65 us -> none  [solve_pairs(): lax.all_to_all(spectrum, 'grid', split_axis=3, concat_axis=2, tiled=True)]
    reduce_sum x1 -> x0, other arithmetic: 7.49 us -> none  [pair_terms(): partner = jnp.sum(potential * owned[None], axis=1)]
  transfers between devices with their start and end apart: 10 -> 0, of which waited for: 9 -> 0; matrix products, arithmetic and copies ran while one was open for 23% -> 0% of each run, Pallas kernels for 0% -> 0%
where the time goes in v1:
time: 259 us
  Pallas kernels  254 us (98%)
  local copies, waits for them, and re-layouts  4.61 us (2%)
    pallas_call x1, Pallas kernels, body(): pl.pallas_call(kernel, out_shape=[jax.ShapeDtypeStruct(own_bands.shape, F...  254 us

profile of v1, /device:TPU:1, one launch (start us, length us, event | category | flops | bytes accessed | tf_op | source)
XLA Modules:
  0.0 258.9 jit_solution(3022794186718074616)
XLA Ops:
  0.6 253.6 %exchange_terms.1 = (f32[4,8,128,128]{3,2,1,0:T(8,128)}, f32[4,8,128,128]{3,2,1,0:T(8,128)}) custom-call(f32[4,8,128,128]{3,2,1,0:T(8,128)} %own.1, f32[4,8,128,128]{3,2,1,0:T(8,128)} %travel.1, bf16[256,256]{1,0:T(8,128)(2,1)} %constant.8.clone.lt_ref, bf16[256,256]{1,0:T(8,128)(2,1)} %constant.9.clone.lti_ref, bf16[256,256]{1,0:T(8,128)(2,1)} %constant.10.clone.wx_ref, ...), custom_call_target="tpu_custom_call" | custom-call | tf_op jit(solution)/shard_map/exchange_terms/pallas_call | solution.py:357
  254.2 0.0 copy-start
  254.3 3.3 %copy.10 = f32[4,8,128,128]{3,2,1,0:T(8,128)} copy(f32[4,8,128,128]{3,2,1,0:T(8,128)} %get-tuple-element.4) | data formatting | bytes 4194304
  257.5 0.0 copy-done
  257.5 1.3 copy.11
Async XLA Ops:
  254.2 3.3 %copy-start = (f32[4,8,128,128]{3,2,1,0:T(8,128)S(1)}, f32[4,8,128,128]{3,2,1,0:T(8,128)}, u32[]{:S(2)}) copy-start(f32[4,8,128,128]{3,2,1,0:T(8,128)} %get-tuple-element.5) | copy-start | bytes 6291460

commit v2 on v1

v2 whole, which is shorter than its diff:
```python
import functools
import math

import jax
import jax.numpy as jnp
import ml_dtypes
import numpy as np
from jax import lax
from jax.experimental import pallas as pl
from jax.experimental.pallas import tpu as pltpu
from jax.sharding import PartitionSpec as P

N = 128
FRACTION = 0.25
ROW = 8
KYS = N // ROW
LOCAL = 8
COLUMN = 8
AHEAD = 1
VIS = 4
PAIRED = 2
BLOCK = LOCAL * KYS
PAIR_ROWS = 2 * ROW * BLOCK
STEPS = ((2, 0), (2, 1), (1, 0), (3, 0), (1, 1), (3, 1), (0, 1))
F32 = jnp.float32
BF16 = jnp.bfloat16
MESH = pl.DeviceIdType.MESH


def real_basis():
    n = np.arange(N)
    rows = []
    for m in range(N):
        if m <= N // 2:
            row = np.cos(2.0 * np.pi * ((m * n) % N) / N)
        else:
            row = np.sin(2.0 * np.pi * (((N - m) * n) % N) / N)
        scale = 1.0 / N if m in (0, N // 2) else 2.0 / N
        rows.append(np.sqrt(scale) * row)
    return np.stack(rows)


def high_low(table):
    high = table.astype(np.float32).astype(ml_dtypes.bfloat16)
    low = (table - high.astype(np.float64)).astype(np.float32).astype(ml_dtypes.bfloat16)
    return high, low


def tables():
    basis = real_basis()
    high, low = high_low(basis)
    high_t, low_t = high.T, low.T
    from_left = np.block([[high, high], [low, low]])
    from_left_inverse = np.block([[high_t, high_t], [low_t, low_t]])
    from_right = np.block([[high_t, low_t], [high_t, low_t]])
    from_right_inverse = np.block([[high, low], [high, low]])
    return [from_left, from_left_inverse, from_right, from_right_inverse]


def halves(value, axis):
    high = value.astype(BF16)
    low = (value - high.astype(F32)).astype(BF16)
    return jnp.concatenate([high, low], axis=axis)


def along_rows(table, value):
    both = jnp.dot(table, halves(value, 0), preferred_element_type=F32)
    return both[:N] + both[N:]


def along_lanes(value, table):
    both = jnp.dot(halves(value, 1), table, preferred_element_type=F32)
    return both[:, :N] + both[:, N:]


def wave_square(position):
    position = lax.rem(position + N // 2, N) - N // 2
    number = 2.0 * math.pi / N * position.astype(F32)
    return number * number


def kernel(
    own, travel, lt_ref, lti_ref, wx_ref, wxi_ref, own_out, held_out,
    ownb, visb, send, recv, back, own_sum, held, held_part, coulomb,
    load_sem, exch_send, exch_recv, vis_send, vis_recv, relay_send, relay_recv,
    fwd_send, fwd_recv, bwd_send, bwd_recv,
    part_send, part_recv, out_send, out_recv, ret_send, ret_recv, store_sem,
):
    band = lax.axis_index("band")
    groups = lax.axis_size("band")
    grid = lax.axis_index("grid")
    mine = grid // ROW
    other = 1 - mine
    place = grid % ROW
    x, core = place // 2, place % 2
    partner = {"grid": other * ROW + place}
    ahead_band = (band + 1) % groups
    turn = (COLUMN - band % COLUMN) // COLUMN
    ahead_turn = (COLUMN - ahead_band % COLUMN) // COLUMN
    direct = (mine + turn) % 2
    passed = 1 - direct
    ahead = {"band": ahead_band, "grid": (mine + ahead_turn) % 2 * ROW + place}
    behind = {"band": (band + groups - 1) % groups, "grid": direct * ROW + place}
    places = [((x + dx) % 4) * 2 + (core + dc) % 2 for dx, dc in STEPS]
    peers = [{"grid": mine * ROW + p} for p in places]

    def remote(src, dst, send_sem, recv_sem, device):
        return pltpu.make_async_remote_copy(
            src_ref=src, dst_ref=dst, send_sem=send_sem, recv_sem=recv_sem,
            device_id=device, device_id_type=MESH,
        )

    for i in range(PAIRED):
        pltpu.make_async_copy(own.at[2 * mine + i], ownb.at[i, mine], load_sem.at[i]).start()

    barrier = pltpu.get_barrier_semaphore()
    for device in [ahead, behind, partner] + peers:
        pl.semaphore_signal(barrier, inc=1, device_id=device, device_id_type=MESH)
    pl.semaphore_wait(barrier, 3 + len(peers))

    def visitor(j, q):
        return remote(
            travel.at[j, pl.ds(2 * q, 2)], visb.at[j, mine, pl.ds(2 * q, 2)],
            vis_send, vis_recv.at[j, q], ahead,
        )

    def relay(j, q, half):
        return remote(
            visb.at[j, half, pl.ds(2 * q, 2)], visb.at[j, half, pl.ds(2 * q, 2)],
            relay_send, relay_recv.at[j, q], partner,
        )

    def exchange(i, q, half, index):
        return remote(
            own.at[index, pl.ds(2 * q, 2)], ownb.at[i, half, pl.ds(2 * q, 2)],
            exch_send, exch_recv.at[i, q], partner,
        )

    def hand_over(i):
        for q in range(4):
            exchange(i, q, mine, 2 * other + i).start()

    for j in range(VIS):
        for q in range(4):
            visitor(j, q).start()

    @pl.when(turn == 0)
    def _():
        hand_over(0)

    kz = lax.broadcasted_iota(jnp.int32, (N, 2 * N), 0)
    lane = lax.broadcasted_iota(jnp.int32, (N, 2 * N), 1)
    kx_square = wave_square(lax.rem(lane, N))
    kz_square = wave_square(kz)

    def fill(kp, carry):
        ky = place * KYS + 2 * kp + lane // N
        squared = kz_square + wave_square(ky) + kx_square
        safe = jnp.where(squared > 0.0, squared, 1.0)
        value = jnp.where(squared > 0.0, 4.0 * math.pi / safe, 0.0)
        coulomb[kp] = -FRACTION * value
        return carry

    lax.fori_loop(0, KYS // 2, fill, 0)

    def base(j, i, half, p):
        return ((j * PAIRED + i) * 2 + half) * ROW * BLOCK + p * BLOCK

    def rows(ref, start, count):
        return ref.at[pl.ds(pl.multiple_of(start, KYS), count)]

    def pass_on(index):
        j, q = index // 4, index % 4
        visitor(j, q).wait_recv()
        relay(j, q, direct).start()

    def transform(j, i, half, q):
        planes = pl.ds(2 * q, 2)
        density = (ownb[i, half, planes] * visb[j, half, planes]).reshape(2 * N, N)
        wave = along_lanes(density, wx_ref[...])
        wave = jnp.concatenate([wave[:N], wave[N:]], axis=1)
        wave = along_rows(lt_ref[...], wave)
        for p in range(ROW):
            for z in range(2):
                start = base(j, i, half, p) + (2 * q + z) * KYS
                send[pl.ds(pl.multiple_of(start, KYS), KYS), :] = wave[
                    p * KYS : (p + 1) * KYS, z * N : (z + 1) * N
                ]
        start = pl.multiple_of(base(j, i, half, place) + 2 * q * KYS, KYS)
        recv[pl.ds(start, 2 * KYS), :] = send[pl.ds(start, 2 * KYS), :]
        for p, peer in zip(places, peers):
            remote(
                rows(send, base(j, i, half, p) + 2 * q * KYS, 2 * KYS),
                rows(recv, base(j, i, half, place) + 2 * q * KYS, 2 * KYS),
                fwd_send, fwd_recv.at[j, half], peer,
            ).start()

    def forward_mine(first, last):
        def piece(step, carry):
            j, q = step // 4, step % 4
            index = step + AHEAD * turn

            @pl.when(index < 4 * VIS)
            def _():
                pass_on(index)

            @pl.when(turn == 1)
            def _():
                relay(j, q, passed).wait_recv()

            for i in range(PAIRED):
                transform(j, i, mine, q)
            return carry

        lax.fori_loop(4 * first, 4 * last, piece, 0)

    def forward_other(visitors, fresh):
        def piece(step, carry):
            i, q = step // 4, step % 4
            if fresh:
                exchange(i, q, other, 2 * mine + i).wait_recv()

            @pl.when((turn == 0) & (i == 0))
            def _():
                for j in visitors:
                    relay(j, q, passed).wait_recv()

            for j in visitors:
                transform(j, i, other, q)
            return carry

        lax.fori_loop(0, 4 * PAIRED, piece, 0)

    def screen(j):
        for half in (mine, other):
            whole = rows(recv, 0, (ROW - 1) * PAIRED * BLOCK)
            remote(whole, whole, fwd_send, fwd_recv.at[j, half], partner).wait_recv()

        def columns(step, carry):
            i, kp = step // (KYS // 2), step % (KYS // 2)
            start = (j * PAIRED + i) * PAIR_ROWS + 2 * kp
            first = pl.ds(start, N, stride=KYS)
            second = pl.ds(start + 1, N, stride=KYS)
            wave = jnp.concatenate([recv[first, :], recv[second, :]], axis=1)
            wave = along_rows(lt_ref[...], wave) * coulomb[kp]
            wave = along_rows(lti_ref[...], wave)
            recv[first, :] = wave[:, :N]
            recv[second, :] = wave[:, N:]
            return carry

        lax.fori_loop(0, PAIRED * KYS // 2, columns, 0)
        for i in range(PAIRED):
            for half in range(2):
                start = pl.multiple_of(base(j, i, half, place), KYS)
                back[pl.ds(start, BLOCK), :] = recv[pl.ds(start, BLOCK), :]

    def give_back(visitors, half):
        def piece(q, carry):
            for j in visitors:
                for i in range(PAIRED):
                    for p, peer in zip(places, peers):
                        remote(
                            rows(recv, base(j, i, half, p) + 2 * q * KYS, 2 * KYS),
                            rows(back, base(j, i, half, place) + 2 * q * KYS, 2 * KYS),
                            bwd_send, bwd_recv.at[j, half, q], peer,
                        ).start()
            return carry

        lax.fori_loop(0, 4, piece, 0)

    def inverse(j, half, q):
        whole = rows(back, 0, (ROW - 1) * PAIRED * 2 * KYS)
        remote(whole, whole, bwd_send, bwd_recv.at[j, half, q], partner).wait_recv()
        planes = pl.ds(2 * q, 2)
        held_term = None
        for i in range(PAIRED):
            sides = []
            for k in range(2):
                parts = []
                for p in range(ROW):
                    start = base(j, i, half, p) + (2 * q + k) * KYS
                    parts.append(back[pl.ds(pl.multiple_of(start, KYS), KYS), :])
                sides.append(jnp.concatenate(parts, axis=0))
            wave = along_rows(lti_ref[...], jnp.concatenate(sides, axis=1))
            wave = jnp.concatenate([wave[:, :N], wave[:, N:]], axis=0)
            potential = along_lanes(wave, wxi_ref[...]).reshape(2, N, N)
            own_part = potential * visb[j, half, planes]
            if j > 0:
                own_part = own_part + own_sum[i, half, planes]
            own_sum[i, half, planes] = own_part
            term = potential * ownb[i, half, planes]
            held_term = term if held_term is None else held_term + term
        held[j, half, planes] = held_term

    def partial(j, q):
        planes = pl.ds(2 * q, 2)
        return remote(
            held.at[j, passed, planes], held_part.at[j, planes],
            part_send, part_recv.at[j, q], partner,
        )

    def outgoing(j, q):
        planes = pl.ds(2 * q, 2)
        return remote(
            held.at[j, direct, planes], held_out.at[j, planes],
            out_send, out_recv, behind,
        )

    def returned(i, q):
        planes = pl.ds(2 * q, 2)
        return remote(
            own_sum.at[i, other, planes], own_out.at[2 * mine + i, planes],
            ret_send, ret_recv, partner,
        )

    def stored(i, q):
        planes = pl.ds(2 * q, 2)
        return pltpu.make_async_copy(
            own_sum.at[i, mine, planes], own_out.at[2 * mine + i, planes], store_sem.at[i, q]
        )

    def settle(j, q):
        partial(j, q).wait_recv()
        planes = pl.ds(2 * q, 2)
        held[j, direct, planes] = held[j, direct, planes] + held_part[j, planes]
        outgoing(j, q).start()

    def back_other(visitors):
        def piece(q, carry):
            for j in visitors:
                inverse(j, other, q)

                @pl.when(turn == 0)
                def _():
                    partial(j, q).start()

            if VIS - 1 in visitors:
                for i in range(PAIRED):
                    returned(i, q).start()
            return carry

        lax.fori_loop(0, 4, piece, 0)

    def back_mine(j):
        def piece(q, carry):
            inverse(j, mine, q)
            if j == VIS - 1:
                for i in range(PAIRED):
                    stored(i, q).start()

            @pl.when(turn == 0)
            def _():
                settle(j, q)

            @pl.when(turn == 1)
            def _():
                partial(j, q).start()
                index = 4 * j + q - 1

                @pl.when(index >= 0)
                def _():
                    settle(index // 4, index % 4)

            return carry

        lax.fori_loop(0, 4, piece, 0)

    @pl.when(turn == 1)
    def _():
        lax.fori_loop(0, AHEAD, lambda index, carry: (pass_on(index), carry)[1], 0)

    for i in range(PAIRED):
        pltpu.make_async_copy(own.at[2 * mine + i], ownb.at[i, mine], load_sem.at[i]).wait()
    forward_mine(0, 2)

    @pl.when(turn == 0)
    def _():
        hand_over(1)

    forward_mine(2, 3)

    @pl.when(turn == 1)
    def _():
        for i in range(PAIRED):
            hand_over(i)

    forward_other([0, 1], True)
    forward_other([2], False)
    screen(0)
    give_back([0], other)

    @pl.when(turn == 1)
    def _():
        give_back([0], mine)

    forward_mine(3, 4)
    forward_other([3], False)
    screen(1)
    give_back([1], other)

    @pl.when(turn == 1)
    def _():
        give_back([1], mine)

    back_other([0])

    @pl.when(turn == 1)
    def _():
        back_mine(0)

    screen(2)
    screen(3)
    give_back([2, 3], other)

    @pl.when(turn == 0)
    def _():
        give_back([0], mine)
        give_back([1], mine)

    give_back([2], mine)
    give_back([3], mine)
    back_other([1])

    @pl.when(turn == 1)
    def _():
        back_mine(1)

    back_other([2, 3])

    @pl.when(turn == 0)
    def _():
        back_mine(0)
        back_mine(1)

    back_mine(2)
    back_mine(3)

    @pl.when(turn == 1)
    def _():
        settle(VIS - 1, 3)

    def all_of(count, send_sem, recv_sem):
        whole = rows(send, 0, count)
        return remote(whole, whole, send_sem, recv_sem, partner)

    row_share = (ROW - 1) * PAIRED * 2 * VIS * BLOCK
    all_of(row_share, fwd_send, out_recv).wait_send()
    all_of(row_share, bwd_send, out_recv).wait_send()
    visit_share, own_share = VIS * LOCAL * N, PAIRED * LOCAL * N
    for sem in (vis_send, relay_send, part_send):
        all_of(visit_share, sem, out_recv).wait_send()
    all_of(own_share, exch_send, out_recv).wait_send()
    all_of(visit_share, out_send, out_recv).wait()
    all_of(own_share, ret_send, ret_recv).wait()
    for i in range(PAIRED):
        for q in range(4):
            stored(i, q).wait()


def body(own_bands, travel_bands):
    table_list = [jnp.asarray(t) for t in tables()]
    whole = 4 * PAIR_ROWS * PAIRED
    dma = pltpu.SemaphoreType.DMA
    any_space = pl.BlockSpec(memory_space=pl.ANY)
    vmem = pl.BlockSpec(memory_space=pltpu.VMEM)
    return pl.pallas_call(
        kernel,
        out_shape=[
            jax.ShapeDtypeStruct(own_bands.shape, F32),
            jax.ShapeDtypeStruct(travel_bands.shape, F32),
        ],
        in_specs=[any_space, any_space] + [vmem] * 4,
        out_specs=[any_space, any_space],
        scratch_shapes=[
            pltpu.VMEM((PAIRED, 2, LOCAL, N, N), F32),
            pltpu.VMEM((VIS, 2, LOCAL, N, N), F32),
            pltpu.VMEM((whole, N), F32),
            pltpu.VMEM((whole, N), F32),
            pltpu.VMEM((whole, N), F32),
            pltpu.VMEM((PAIRED, 2, LOCAL, N, N), F32),
            pltpu.VMEM((VIS, 2, LOCAL, N, N), F32),
            pltpu.VMEM((VIS, LOCAL, N, N), F32),
            pltpu.VMEM((KYS // 2, N, 2 * N), F32),
            dma((PAIRED,)),
            dma,
            dma((PAIRED, 4)),
            dma,
            dma((VIS, 4)),
            dma,
            dma((VIS, 4)),
            dma,
            dma((VIS, 2)),
            dma,
            dma((VIS, 2, 4)),
            dma,
            dma((VIS, 4)),
            dma,
            dma,
            dma,
            dma,
            dma((PAIRED, 4)),
        ],
        compiler_params=pltpu.CompilerParams(
            collective_id=0, has_side_effects=True, vmem_limit_bytes=46 * 2**20
        ),
        name="exchange_terms",
    )(own_bands, travel_bands, *table_list)


def solution(mesh):
    in_specs = (P("band", "grid", None, None), P("band", "grid", None, None))
    out_specs = (P("band", "grid", None, None), P("band", "grid", None, None))
    return jax.shard_map(body, mesh=mesh, in_specs=in_specs, out_specs=out_specs, check_vma=False)
```

time: 259 us -> 227 us (0.88)
  Pallas kernels: 254 us -> 218 us
  local copies, waits for them, and re-layouts: 4.61 us -> 7.84 us
    pallas_call x1, Pallas kernels: 254 us -> 218 us  [body(): pl.pallas_call(kernel, out_shape=[jax.ShapeDtypeStruct(own_bands.shape, F...]
    unnamed x4 -> x12, local copies, waits for them, and re-layouts: 4.61 us -> 7.84 us
where the time goes in v2:
time: 227 us
  Pallas kernels  218 us (96%)
  local copies, waits for them, and re-layouts  7.84 us (3%)
    pallas_call x1, Pallas kernels, body(): pl.pallas_call(kernel, out_shape=[jax.ShapeDtypeStruct(own_bands.shape, F...  218 us
    unnamed x12, local copies, waits for them, and re-layouts  7.84 us

profile of v2, /device:TPU:1, one launch (start us, length us, event | category | flops | bytes accessed | tf_op | source)
XLA Modules:
  0.0 226.7 jit_solution(2885987386257851790)
XLA Ops:
  0.6 0.0 copy-start
  0.6 1.6 copy-done
  2.2 0.0 copy-start.1
  2.2 0.9 copy-done.1
  3.1 0.0 copy-start.2
  3.1 0.9 copy-done.2
  4.0 0.0 copy-start.3
  4.0 0.9 copy-done.3
  4.9 0.0 copy-start.4
  4.9 0.9 copy-done.4
  5.8 218.2 %exchange_terms.1 = (f32[4,8,128,128]{3,2,1,0:T(8,128)S(1)}, f32[4,8,128,128]{3,2,1,0:T(8,128)S(1)}) custom-call(f32[4,8,128,128]{3,2,1,0:T(8,128)S(1)} %copy-done, f32[4,8,128,128]{3,2,1,0:T(8,128)} %travel.1, bf16[256,256]{1,0:T(8,128)(2,1)S(1)} %copy-done.4, bf16[256,256]{1,0:T(8,128)(2,1)S(1)} %copy-done.3, bf16[256,256]{1,0:T(8,128)(2,1)S(1)} %copy-done.2, ...), custom_call_target="tpu_custom_call" | custom-call | tf_op jit(solution)/shard_map/exchange_terms/pallas_call | solution.py:466
  224.1 1.3 copy.10
  225.4 1.3 copy.11
Async XLA Ops:
  0.6 1.6 copy-start
  2.2 0.9 copy-start.1
  3.1 0.9 copy-start.2
  4.0 0.9 copy-start.3
  4.9 0.9 copy-start.4

commit v3 on v2

--- a/solution.py
+++ b/solution.py
@@ -80,9 +80,9 @@
 
 
 def kernel(
-    own, travel, lt_ref, lti_ref, wx_ref, wxi_ref, own_out, held_out,
+    own, travel, tables_in, own_out, held_out, table,
     ownb, visb, send, recv, back, own_sum, held, held_part, coulomb,
-    load_sem, exch_send, exch_recv, vis_send, vis_recv, relay_send, relay_recv,
+    table_sem, load_sem, exch_send, exch_recv, vis_send, vis_recv, relay_send, relay_recv,
     fwd_send, fwd_recv, bwd_send, bwd_recv,
     part_send, part_recv, out_send, out_recv, ret_send, ret_recv, store_sem,
 ):
@@ -110,6 +110,8 @@
             device_id=device, device_id_type=MESH,
         )
 
+    lt_ref, lti_ref, wx_ref, wxi_ref = (table.at[n] for n in range(4))
+    pltpu.make_async_copy(tables_in, table, table_sem).start()
     for i in range(PAIRED):
         pltpu.make_async_copy(own.at[2 * mine + i], ownb.at[i, mine], load_sem.at[i]).start()
 
@@ -348,18 +350,15 @@
                 for i in range(PAIRED):
                     stored(i, q).start()
 
-            @pl.when(turn == 0)
-            def _():
-                settle(j, q)
-
             @pl.when(turn == 1)
             def _():
                 partial(j, q).start()
-                index = 4 * j + q - 1
-
-                @pl.when(index >= 0)
-                def _():
-                    settle(index // 4, index % 4)
+
+            index = 4 * j + q - turn
+
+            @pl.when(index >= 0)
+            def _():
+                settle(index // 4, index % 4)
 
             return carry
 
@@ -369,6 +368,7 @@
     def _():
         lax.fori_loop(0, AHEAD, lambda index, carry: (pass_on(index), carry)[1], 0)
 
+    pltpu.make_async_copy(tables_in, table, table_sem).wait()
     for i in range(PAIRED):
         pltpu.make_async_copy(own.at[2 * mine + i], ownb.at[i, mine], load_sem.at[i]).wait()
     forward_mine(0, 2)
@@ -458,20 +458,20 @@
 
 
 def body(own_bands, travel_bands):
-    table_list = [jnp.asarray(t) for t in tables()]
+    table_stack = jnp.asarray(np.stack(tables()))
     whole = 4 * PAIR_ROWS * PAIRED
     dma = pltpu.SemaphoreType.DMA
     any_space = pl.BlockSpec(memory_space=pl.ANY)
-    vmem = pl.BlockSpec(memory_space=pltpu.VMEM)
     return pl.pallas_call(
         kernel,
         out_shape=[
             jax.ShapeDtypeStruct(own_bands.shape, F32),
             jax.ShapeDtypeStruct(travel_bands.shape, F32),
         ],
-        in_specs=[any_space, any_space] + [vmem] * 4,
+        in_specs=[any_space] * 3,
         out_specs=[any_space, any_space],
         scratch_shapes=[
+            pltpu.VMEM((4, 2 * N, 2 * N), BF16),
             pltpu.VMEM((PAIRED, 2, LOCAL, N, N), F32),
             pltpu.VMEM((VIS, 2, LOCAL, N, N), F32),
             pltpu.VMEM((whole, N), F32),
@@ -481,6 +481,7 @@
             pltpu.VMEM((VIS, 2, LOCAL, N, N), F32),
             pltpu.VMEM((VIS, LOCAL, N, N), F32),
             pltpu.VMEM((KYS // 2, N, 2 * N), F32),
+            dma,
             dma((PAIRED,)),
             dma,
             dma((PAIRED, 4)),
@@ -501,10 +502,10 @@
             dma((PAIRED, 4)),
         ],
         compiler_params=pltpu.CompilerParams(
-            collective_id=0, has_side_effects=True, vmem_limit_bytes=46 * 2**20
+            collective_id=0, has_side_effects=True, vmem_limit_bytes=49 * 2**20
         ),
         name="exchange_terms",
-    )(own_bands, travel_bands, *table_list)
+    )(own_bands, travel_bands, table_stack)
 
 
 def solution(mesh):

time: 227 us -> 223 us (0.982)
  local copies, waits for them, and re-layouts: 7.84 us -> 3.68 us
    unnamed x12 -> x4, local copies, waits for them, and re-layouts: 7.84 us -> 3.68 us
where the time goes in v3:
time: 223 us; the launch traced here: 222 us
  Pallas kernels  218 us (98%)
  local copies, waits for them, and re-layouts  3.68 us (2%)
    pallas_call x1, Pallas kernels, body(): pl.pallas_call(kernel, out_shape=[jax.ShapeDtypeStruct(own_bands.shape, F...  218 us

profile of v3, /device:TPU:1, one launch (start us, length us, event | category | flops | bytes accessed | tf_op | source)
XLA Modules:
  0.0 222.5 jit_solution(7398857532839342456)
XLA Ops:
  0.6 0.0 copy-start
  0.6 1.0 copy-done
  1.7 218.1 %exchange_terms.1 = (f32[4,8,128,128]{3,2,1,0:T(8,128)S(1)}, f32[4,8,128,128]{3,2,1,0:T(8,128)S(1)}) custom-call(f32[4,8,128,128]{3,2,1,0:T(8,128)} %own.1, f32[4,8,128,128]{3,2,1,0:T(8,128)} %travel.1, bf16[4,256,256]{2,1,0:T(8,128)(2,1)S(1)} %copy-done), custom_call_target="tpu_custom_call" | custom-call | tf_op jit(solution)/shard_map/exchange_terms/pallas_call | solution.py:465
  219.8 1.3 copy.7
  221.2 1.3 copy.8
Async XLA Ops:
  0.6 1.0 copy-start

commit v4 on v3

--- a/solution.py
+++ b/solution.py
@@ -16,7 +16,6 @@
 KYS = N // ROW
 LOCAL = 8
 COLUMN = 8
-AHEAD = 1
 VIS = 4
 PAIRED = 2
 BLOCK = LOCAL * KYS
@@ -150,6 +149,12 @@
     def _():
         hand_over(0)
 
+    @pl.when(turn == 1)
+    def _():
+        for q in range(4):
+            for i in range(PAIRED):
+                exchange(i, q, mine, 2 * other + i).start()
+
     kz = lax.broadcasted_iota(jnp.int32, (N, 2 * N), 0)
     lane = lax.broadcasted_iota(jnp.int32, (N, 2 * N), 1)
     kx_square = wave_square(lax.rem(lane, N))
@@ -200,21 +205,61 @@
     def forward_mine(first, last):
         def piece(step, carry):
             j, q = step // 4, step % 4
-            index = step + AHEAD * turn
-
-            @pl.when(index < 4 * VIS)
+            pass_on(step)
+            for i in range(PAIRED):
+                transform(j, i, mine, q)
+            return carry
+
+        lax.fori_loop(4 * first, 4 * last, piece, 0)
+
+    def turned_start():
+        def piece(q, carry):
+            pass_on(q)
+            for i in range(PAIRED):
+                exchange(i, q, other, 2 * mine + i).wait_recv()
+                transform(0, i, other, q)
+
+            @pl.when(q > 0)
             def _():
-                pass_on(index)
-
-            @pl.when(turn == 1)
+                straight(q + 3, 0)
+
+            return carry
+
+        def straight(step, carry):
+            pass_on(step)
+            for i in range(PAIRED):
+                transform(step // 4, i, other, step % 4)
+            return carry
+
+        def own_planes(step, carry):
+            relay(step // 4, step % 4, passed).wait_recv()
+            for i in range(PAIRED):
+                transform(step // 4, i, mine, step % 4)
+            return carry
+
+        lax.fori_loop(0, 4, piece, 0)
+        lax.fori_loop(7, 12, straight, 0)
+        lax.fori_loop(0, 12, own_planes, 0)
+
+    def turned(first, last):
+        def own_planes(step):
+            relay(step // 4, step % 4, passed).wait_recv()
+            for i in range(PAIRED):
+                transform(step // 4, i, mine, step % 4)
+
+        def piece(step, carry):
+            pass_on(step)
+            for i in range(PAIRED):
+                transform(step // 4, i, other, step % 4)
+
+            @pl.when(step > 4 * first)
             def _():
-                relay(j, q, passed).wait_recv()
-
-            for i in range(PAIRED):
-                transform(j, i, mine, q)
+                own_planes(step - 1)
+
             return carry
 
         lax.fori_loop(4 * first, 4 * last, piece, 0)
+        own_planes(4 * last - 1)
 
     def forward_other(visitors, fresh):
         def piece(step, carry):
@@ -222,7 +267,7 @@
             if fresh:
                 exchange(i, q, other, 2 * mine + i).wait_recv()
 
-            @pl.when((turn == 0) & (i == 0))
+            @pl.when(i == 0)
             def _():
                 for j in visitors:
                     relay(j, q, passed).wait_recv()
@@ -327,117 +372,82 @@
         held[j, direct, planes] = held[j, direct, planes] + held_part[j, planes]
         outgoing(j, q).start()
 
-    def back_other(visitors):
+    def back_other(visitors, turned_here):
         def piece(q, carry):
             for j in visitors:
                 inverse(j, other, q)
-
-                @pl.when(turn == 0)
-                def _():
+                if not turned_here:
                     partial(j, q).start()
-
             if VIS - 1 in visitors:
                 for i in range(PAIRED):
                     returned(i, q).start()
+            if turned_here:
+                for j in visitors:
+                    settle(j, q)
             return carry
 
         lax.fori_loop(0, 4, piece, 0)
 
-    def back_mine(j):
+    def back_mine(j, turned_here):
         def piece(q, carry):
             inverse(j, mine, q)
+            if turned_here:
+                partial(j, q).start()
+            else:
+                settle(j, q)
             if j == VIS - 1:
                 for i in range(PAIRED):
                     stored(i, q).start()
-
-            @pl.when(turn == 1)
-            def _():
-                partial(j, q).start()
-
-            index = 4 * j + q - turn
-
-            @pl.when(index >= 0)
-            def _():
-                settle(index // 4, index % 4)
-
             return carry
 
         lax.fori_loop(0, 4, piece, 0)
-
-    @pl.when(turn == 1)
-    def _():
-        lax.fori_loop(0, AHEAD, lambda index, carry: (pass_on(index), carry)[1], 0)
 
     pltpu.make_async_copy(tables_in, table, table_sem).wait()
     for i in range(PAIRED):
         pltpu.make_async_copy(own.at[2 * mine + i], ownb.at[i, mine], load_sem.at[i]).wait()
-    forward_mine(0, 2)
-
     @pl.when(turn == 0)
     def _():
+        forward_mine(0, 2)
         hand_over(1)
-
-    forward_mine(2, 3)
+        forward_mine(2, 3)
+        forward_other([0, 1], True)
+        forward_other([2], False)
+        screen(0)
+        give_back([0], other)
+        forward_mine(3, 4)
+        forward_other([3], False)
+        screen(1)
+        give_back([1], other)
+        back_other([0], False)
+        screen(2)
+        screen(3)
+        give_back([2, 3], other)
+        for j in range(VIS):
+            give_back([j], mine)
+        back_other([1], False)
+        back_other([2, 3], False)
+        for j in range(VIS):
+            back_mine(j, False)
 
     @pl.when(turn == 1)
     def _():
-        for i in range(PAIRED):
-            hand_over(i)
-
-    forward_other([0, 1], True)
-    forward_other([2], False)
-    screen(0)
-    give_back([0], other)
-
-    @pl.when(turn == 1)
-    def _():
+        turned_start()
+        screen(0)
         give_back([0], mine)
-
-    forward_mine(3, 4)
-    forward_other([3], False)
-    screen(1)
-    give_back([1], other)
-
-    @pl.when(turn == 1)
-    def _():
+        give_back([0], other)
+        turned(3, 4)
+        screen(1)
         give_back([1], mine)
-
-    back_other([0])
-
-    @pl.when(turn == 1)
-    def _():
-        back_mine(0)
-
-    screen(2)
-    screen(3)
-    give_back([2, 3], other)
-
-    @pl.when(turn == 0)
-    def _():
-        give_back([0], mine)
-        give_back([1], mine)
-
-    give_back([2], mine)
-    give_back([3], mine)
-    back_other([1])
-
-    @pl.when(turn == 1)
-    def _():
-        back_mine(1)
-
-    back_other([2, 3])
-
-    @pl.when(turn == 0)
-    def _():
-        back_mine(0)
-        back_mine(1)
-
-    back_mine(2)
-    back_mine(3)
-
-    @pl.when(turn == 1)
-    def _():
-        settle(VIS - 1, 3)
+        back_mine(0, True)
+        screen(2)
+        give_back([2], mine)
+        back_other([0], True)
+        screen(3)
+        give_back([3], mine)
+        give_back([1, 2, 3], other)
+        for j in range(1, VIS):
+            back_mine(j, True)
+        back_other([1, 2, 3], True)
 
     def all_of(count, send_sem, recv_sem):
         whole = rows(send, 0, count)

time: 223 us -> 221 us (level)
  no operation moved by 1% of the time
where the time goes in v4:
time: 221 us; the launch traced here: 220 us
  Pallas kernels  216 us (98%)
  local copies, waits for them, and re-layouts  3.68 us (2%)
    pallas_call x1, Pallas kernels, body(): pl.pallas_call(kernel, out_shape=[jax.ShapeDtypeStruct(own_bands.shape, F...  216 us

profile of v4, /device:TPU:1, one launch (start us, length us, event | category | flops | bytes accessed | tf_op | source)
XLA Modules:
  0.0 220.4 jit_solution(10406652994467813367)
XLA Ops:
  0.6 0.0 copy-start
  0.6 1.0 copy-done
  1.7 216.1 %exchange_terms.1 = (f32[4,8,128,128]{3,2,1,0:T(8,128)S(1)}, f32[4,8,128,128]{3,2,1,0:T(8,128)S(1)}) custom-call(f32[4,8,128,128]{3,2,1,0:T(8,128)} %own.1, f32[4,8,128,128]{3,2,1,0:T(8,128)} %travel.1, bf16[4,256,256]{2,1,0:T(8,128)(2,1)S(1)} %copy-done), custom_call_target="tpu_custom_call" | custom-call | tf_op jit(solution)/shard_map/exchange_terms/pallas_call | solution.py:475
  217.7 1.3 copy.7
  219.1 1.3 copy.8
Async XLA Ops:
  0.6 1.0 copy-start
